TPU v7x, 128 devices: a whole 4x4x4 slice. The times are simulated.
128 devices in a mesh: fsdp: 16 (over y_hi, z, core), tensor: 8 (over y_lo, x).
Axes of the slice: x: 4, y: 4 (y_hi: 2, y_lo: 2; y = y_hi * 2 + y_lo), z: 4, core: 2. Of those that a mesh axis runs over, the one named last changes fastest.
Arguments:
- states: bfloat16 [4096, 8192], P('fsdp'), may hold values from -64 to 64
- segment_ids: int32 [16, 256], P('fsdp'), may hold values from 0 to 3, never falling along the last dimension, each value on 1 to 128 neighbouring positions
- attn_gain: float32 [8192], replicated, may hold values from 0.1 to 1.9
- query_weight: bfloat16 [8192, 4096], P('fsdp', 'tensor'), may hold values from -2 to 2
- key_weight: bfloat16 [8192, 1024], P('fsdp', 'tensor'), may hold values from -2 to 2
- value_matrix: bfloat16 [8192, 1024], P('fsdp', 'tensor'), may hold values from -0.0625 to 0.0625
- out_weight: bfloat16 [4096, 8192], P('tensor', 'fsdp'), may hold values from -0.28125 to 0.28125
- final_gain: float32 [8192], P('tensor'), may hold values from 0.1 to 1.9
- head_weight: float32 [8192], P('tensor'), may hold values from -0.0625 to 0.0625
Outputs:
- scores: float32 [4096], P(('fsdp', 'tensor'))
- resid_out: bfloat16 [4096, 8192], P('fsdp', 'tensor')
Inputs may be any that keep to these rules, and one draw needn't show every extreme that they name: `segment_ids`: in each row, segment numbers never fall and each rollout spans 1 to 128 positions.
All inputs are finite; a program needn't handle non-finite values.
Results may differ from a plain program's by a relative error of at most 0.0071.
Values may be sent and summed in bfloat16 or wider, within the bound.
A program may use at most 128 MiB of HBM per device.

v0:
```python
import jax
import jax.numpy as jnp
from jax import lax
from jax.sharding import PartitionSpec as P

MODEL_WIDTH = 8192
HEAD_SIZE = 128
EPS = 1e-05
THETA = 500000.0
NEG_FILL = -1e30


def in_one_piece(arrays, axis, dim, along):
    both = jnp.concatenate(arrays, axis=along)
    result, at, outs = (lax.all_gather(both, axis, axis=dim, tiled=True), 0, [])
    for a in arrays:
        outs.append(lax.slice_in_dim(result, at, at + a.shape[along], axis=along))
        at += a.shape[along]
    return tuple(outs)


def sent_to_all(value, axis):
    length = lax.axis_size(axis)
    return lax.all_to_all(
        jnp.broadcast_to(value[None], (length, *value.shape)), axis, 0, 0, tiled=True
    )


def over_copies(value, axis):
    return sent_to_all(value, axis).sum(axis=0)


def together(arrays, axis):
    ravelled, at, outs = (jnp.concatenate([a.reshape(-1) for a in arrays]), 0, [])
    total = over_copies(ravelled, axis)
    for a in arrays:
        outs.append(total[at : at + a.size].reshape(a.shape))
        at += a.size
    return tuple(outs)


def rope_tables(seg_row):
    count = seg_row.shape[0]
    places = jnp.arange(count, dtype=jnp.int32)
    boundary = jnp.concatenate([jnp.ones((1,), dtype=bool), seg_row[1:] != seg_row[:-1]])
    begins = lax.cummax(jnp.where(boundary, places, jnp.zeros_like(places)), axis=0)
    positions = (places - begins).astype(jnp.float32)
    half_width = HEAD_SIZE // 2
    frequency = THETA ** (-(2.0 * jnp.arange(half_width, dtype=jnp.float32)) / HEAD_SIZE)
    angles = positions[:, None] * frequency[None, :]
    return (jnp.cos(angles), jnp.sin(angles))


def rotated(block, cosine, sine_part):
    half_width = block.shape[-1] // 2
    first_half = block[..., :half_width]
    second_half = block[..., half_width:]
    cos_rows = cosine[:, None, :]
    sin_rows = sine_part[:, None, :]
    return jnp.concatenate(
        [
            first_half * cos_rows - second_half * sin_rows,
            second_half * cos_rows + first_half * sin_rows,
        ],
        axis=-1,
    )


def attend(queries, key_rows, values, seg_row):
    t_rows = queries.shape[0]
    heads_here = queries.shape[1] // HEAD_SIZE
    groups_here = key_rows.shape[1] // HEAD_SIZE
    ratio = heads_here // groups_here
    cosine, sine_part = rope_tables(seg_row)
    query_rot = rotated(queries.reshape(t_rows, heads_here, HEAD_SIZE), cosine, sine_part).astype(
        jnp.bfloat16
    )
    key_rot = rotated(key_rows.reshape(t_rows, groups_here, HEAD_SIZE), cosine, sine_part).astype(
        jnp.bfloat16
    )
    value_rows = values.astype(jnp.bfloat16).reshape(t_rows, groups_here, HEAD_SIZE)
    grouped = query_rot.reshape(t_rows, groups_here, ratio, HEAD_SIZE)
    logits = jnp.einsum(
        "tkgd,skd->kgts", grouped, key_rot, preferred_element_type=jnp.float32
    ) * HEAD_SIZE ** (-0.5)
    places = jnp.arange(t_rows, dtype=jnp.int32)
    allowed = (seg_row[:, None] == seg_row[None, :]) & (places[None, :] <= places[:, None])
    logits = jnp.where(allowed[None, None], logits, NEG_FILL)
    row_peak = jnp.max(logits, axis=-1, keepdims=True)
    raised = jnp.exp(logits - row_peak)
    probabilities = (raised / jnp.sum(raised, axis=-1, keepdims=True)).astype(jnp.bfloat16)
    mixed = jnp.einsum(
        "kgts,skd->tkgd", probabilities, value_rows, preferred_element_type=jnp.float32
    )
    return mixed.astype(jnp.bfloat16).reshape(t_rows, heads_here * HEAD_SIZE)


def body(
    states,
    segment_ids,
    attn_gain,
    query_weight,
    key_weight,
    value_matrix,
    out_weight,
    final_gain,
    head_weight,
):
    t_rows, width = states.shape
    tensor_count = lax.axis_size("tensor")
    tensor_index = lax.axis_index("tensor")
    widened = states.astype(jnp.float32)
    normed = (
        widened
        * lax.rsqrt(jnp.sum(widened * widened, axis=1, keepdims=True) / MODEL_WIDTH + EPS)
        * attn_gain[None, :]
    ).astype(jnp.bfloat16)

    def add_piece(portion):
        return jnp.dot(normed, portion, preferred_element_type=jnp.float32)

    pieces = in_one_piece((query_weight, key_weight, value_matrix), "fsdp", 0, 1)
    queries = add_piece(pieces[0])
    key_rows = add_piece(pieces[1])
    values = add_piece(pieces[2])
    mixed = attend(queries, key_rows, values, segment_ids[0])
    slice_cols = width // tensor_count
    partials = jnp.dot(
        mixed,
        lax.all_gather(out_weight, "fsdp", axis=1, tiled=True),
        preferred_element_type=jnp.float32,
    )
    branch = lax.psum_scatter(partials, "tensor", scatter_dimension=1, tiled=True)
    own_cols = lax.dynamic_slice_in_dim(widened, tensor_index * slice_cols, slice_cols, 1)
    resid_out = (own_cols + branch).astype(jnp.bfloat16)
    stream = resid_out.astype(jnp.float32)
    squares = jnp.sum(stream * stream, axis=1)
    products = jnp.sum(stream * (final_gain * head_weight)[None, :], axis=1)
    share_rows = t_rows // tensor_count
    squares_all, products_all = together((squares, products), "tensor")
    local_squares = lax.dynamic_slice_in_dim(squares_all, tensor_index * share_rows, share_rows, 0)
    products_mine = lax.dynamic_slice_in_dim(products_all, tensor_index * share_rows, share_rows, 0)
    scores = products_mine * lax.rsqrt(local_squares / MODEL_WIDTH + EPS)
    return (scores, resid_out)


def solution(mesh):
    placed = (
        P("fsdp", None),
        P("fsdp", None),
        P(),
        P("fsdp", "tensor"),
        P("fsdp", "tensor"),
        P("fsdp", "tensor"),
        P("tensor", "fsdp"),
        P("tensor"),
        P("tensor"),
    )
    return jax.shard_map(
        body,
        mesh=mesh,
        in_specs=placed,
        out_specs=(P(("fsdp", "tensor")), P("fsdp", "tensor")),
        check_vma=False,
    )
```

profile of v0, /device:TPU:0, one launch (start us, length us, event | category | flops | bytes accessed | tf_op | source)
XLA Modules:
  0.0 299.0 jit_solution(9830881361931489665)
XLA Ops:
  7.2 0.0 all-gather.3.cloned.1.call-start
  7.2 2.1 pad_maximum_fusion
  9.3 0.0 all-gather.3.cloned.1.call-update
  9.4 0.0 all-gather.5.cloned.1.call-start
  9.4 0.7 all-gather.5.cloned.1.call-update
  10.1 0.0 reduce-scatter.2.cloned.1.call-start
  10.2 0.8 compare_reduce_fusion
  11.0 0.1 fusion.40
  11.1 0.3 reduce-window.9
  11.4 0.1 slice.47
  11.5 0.1 slice_reduce_fusion
  11.6 3.1 %multiply_reduce_fusion = f32[256]{0:T(256)S(1)} fusion(bf16[256,8192]{1,0:T(8,128)(2,1)} %param.9), kind=kLoop, calls=%fused_computation.3 | loop fusion | flops 6291200 | bytes 4195328 | tf_op jit(solution)/shard_map/reduce_sum | solution.py:115
  14.8 0.1 fusion.41
  14.8 0.9 fusion.27
  15.7 0.5 multiply_cosine_fusion
  16.2 0.0 copy-start.2
  16.2 87.3 %all-gather.3.cloned.1.call-done = bf16[8192,768]{1,0:T(8,128)(2,1)} async-done(((bf16[512,768]{1,0:T(8,128)(2,1)}), bf16[8192,768]{1,0:T(8,128)(2,1)}) %all-gather.3.cloned.1.call-update) | async-done | bytes 12582928 | tf_op jit(solution)/shard_map/all_gather | solution.py:15
  103.6 7.1 %fusion = f32[256,512]{1,0:T(8,128)S(1)} fusion(bf16[8192,768]{1,0:T(8,128)(2,1)} %all-gather.3.cloned.1.call-done, f32[8192]{0:T(1024)} %param.11, f32[256]{0:T(256)S(1)} %add_rsqrt_fusion, bf16[256,8192]{1,0:T(8,128)(2,1)} %param.9), kind=kOutput, calls=%fused_computation | convolution fusion | flops 2155872256 | bytes 13140992 | tf_op jit(solution)/shard_map/dot_general | solution.py:120
  110.6 0.2 reshape.251
  110.8 0.0 copy-done.2
  110.8 4.9 %fusion.8 = f32[256,1,128]{0,2,1:T(8,128)S(1)} fusion(bf16[8192,768]{1,0:T(8,128)(2,1)} %all-gather.3.cloned.1.call-done, f32[8192]{0:T(1024)S(1)} %copy-done.2, f32[256]{0:T(256)S(1)} %add_rsqrt_fusion, bf16[256,8192]{1,0:T(8,128)(2,1)} %param.9), kind=kOutput, calls=%fused_computation.14 | convolution fusion | flops 545259520 | bytes 6456320 | tf_op jit(solution)/shard_map/dot_general | solution.py:120
  115.7 0.3 fusion.39
  116.0 0.3 fusion.43
  116.4 0.1 subtract_convert_fusion
  116.5 0.4 fusion.45
  117.0 0.2 fusion.21
  117.1 4.6 %convolution_convert_fusion = bf16[128,4,256]{2,0,1:T(8,128)(2,1)S(1)} fusion(bf16[8192,768]{1,0:T(8,128)(2,1)} %all-gather.3.cloned.1.call-done, f32[1,4,256,256]{2,3,1,0:T(8,128)S(1)} %get-tuple-element.16, f32[4,256]{1,0:T(4,128)S(1)} %fusion.21, f32[4,256]{1,0:T(4,128)S(1)} %get-tuple-element.15, f32[8192]{0:T(1024)S(1)} %copy-done.2, ...), kind=kOutput, calls=%fused_computation.13 | convolution fusion | flops 613318656 | bytes 7644160 | tf_op jit(solution)/shard_map/kgts,skd->tkgd/dot_general | solution.py:92
  121.7 58.3 %all-gather.5.cloned.1.call-done = bf16[512,8192]{1,0:T(8,128)(2,1)} async-done(((bf16[512,512]{1,0:T(8,128)(2,1)}), bf16[512,8192]{1,0:T(8,128)(2,1)}) %all-gather.5.cloned.1.call-update) | async-done | bytes 8388624 | tf_op jit(solution)/shard_map/all_gather | solution.py:130
  180.0 9.0 %fusion.46 = f32[256,8192]{1,0:T(8,128)} fusion(bf16[256,512]{0,1:T(8,128)(2,1)S(1)} %bitcast.40, bf16[512,8192]{1,0:T(8,128)(2,1)} %all-gather.5.cloned.1.call-done), kind=kOutput, calls=%fused_computation.64 | convolution fusion | flops 2147483648 | bytes 17039360 | tf_op jit(solution)/shard_map/dot_general | solution.py:128
  189.0 0.0 reduce-scatter.2.cloned.1.call-update
  189.0 0.0 copy-start
  189.1 0.0 copy-start.1
  189.1 6.7 %convert_element_type.41 = f32[256,8192]{1,0:T(8,128)} convert(bf16[256,8192]{1,0:T(8,128)(2,1)} %param.9) | non-fusion elementwise | flops 2097152 | bytes 12582912 | tf_op jit(solution)/shard_map/convert_element_type | solution.py:112
  195.7 0.0 copy-done
  195.7 0.0 copy-done.1
  195.7 83.5 %reduce-scatter.2.cloned.1.call-done = f32[256,1024]{1,0:T(8,128)} async-done(((f32[256,8192]{1,0:T(8,128)}), f32[256,1024]{1,0:T(8,128)}) %reduce-scatter.2.cloned.1.call-update) | async-done | bytes 1048592 | tf_op jit(solution)/shard_map/reduce_scatter | solution.py:133
  279.2 2.5 fusion.19
  281.8 0.6 broadcast_in_dim.15
  282.4 3.3 %all-to-all-start = ((f32[8,1,512]{2,1,0:T(1,128)}), f32[8,1,512]{2,1,0:T(1,128)S(1)}, u32[]{:S(2)}, u32[]{:S(2)}) async-start(f32[8,1,512]{2,1,0:T(1,128)} %broadcast_in_dim.15), calls=%async_computation.1 | async-start | bytes 32768 | tf_op jit(solution)/shard_map/all_to_all | solution.py:24
  285.7 6.1 %all-to-all-done = f32[8,1,512]{2,1,0:T(1,128)S(1)} async-done(((f32[8,1,512]{2,1,0:T(1,128)}), f32[8,1,512]{2,1,0:T(1,128)S(1)}, u32[]{:S(2)}, u32[]{:S(2)}) %all-to-all-start) | async-done | bytes 16416 | tf_op jit(solution)/shard_map/all_to_all | solution.py:24
  291.9 0.6 rsqrt_multiply_fusion
  (7 shorter events, 0.1 us)
Async XLA Ops:
  7.2 96.4 %all-gather.3.cloned.1.call-start = ((), (), s32[]{:S(2)}) async-start(), calls=%async_computation.2 | async-start | bytes 13369344 | tf_op jit(solution)/shard_map/all_gather | solution.py:15
  9.4 170.7 %all-gather.5.cloned.1.call-start = ((), (), s32[]{:S(2)}) async-start(), calls=%async_computation.3 | async-start | bytes 8912896 | tf_op jit(solution)/shard_map/all_gather | solution.py:130
  10.1 269.1 %reduce-scatter.2.cloned.1.call-start = ((), (), s32[]{:S(2)}) async-start(), calls=%async_computation.4 | async-start | bytes 9437184 | tf_op jit(solution)/shard_map/reduce_scatter | solution.py:133
  16.2 94.6 %copy-start.2 = (f32[8192]{0:T(1024)S(1)}, f32[8192]{0:T(1024)}, u32[]{:S(2)}) copy-start(f32[8192]{0:T(1024)} %param.11) | copy-start | bytes 98308
  189.0 6.7 %copy-start = (f32[1024]{0:T(1024)S(1)}, f32[1024]{0:T(1024)}, u32[]{:S(2)}) copy-start(f32[1024]{0:T(1024)} %param.16) | copy-start | bytes 12292
  189.1 6.7 %copy-start.1 = (f32[1024]{0:T(1024)S(1)}, f32[1024]{0:T(1024)}, u32[]{:S(2)}) copy-start(f32[1024]{0:T(1024)} %param.17) | copy-start | bytes 12292
  282.4 9.5 %all-to-all-start = ((f32[8,1,512]{2,1,0:T(1,128)}), f32[8,1,512]{2,1,0:T(1,128)S(1)}, u32[]{:S(2)}, u32[]{:S(2)}) async-start(f32[8,1,512]{2,1,0:T(1,128)} %broadcast_in_dim.15), calls=%async_computation.1 | async-start | bytes 32768 | tf_op jit(solution)/shard_map/all_to_all | solution.py:24
Sparse Core Ops, SparseCore 0:
  10.5 93.0 all-gather.2
  105.8 74.1 all-gather.4
  189.2 90.0 reduce-scatter.1
where the time goes:
time: 299 us
  waiting for transfers between devices  236 us (79%)
  matrix products  25.9 us (9%)
  other arithmetic  18.4 us (6%)
  between operations  13.9 us (5%)
  starting transfers between devices  3.45 us (1%)
    all_gather x1, waiting for transfers between devices, in_one_piece(): result, at, outs = (lax.all_gather(both, axis, axis=dim, tiled=True), 0, [])  87.3 us
    reduce_scatter x1, waiting for transfers between devices, body(): lax.psum_scatter(partials, 'tensor', scatter_dimension=1, tiled=True)  83.5 us
    all_gather x1, waiting for transfers between devices, body(): lax.all_gather(out_weight, 'fsdp', axis=1, tiled=True)  58.3 us
    dot_general x2, matrix products, add_piece(): return jnp.dot(normed, portion, preferred_element_type=jnp.float32)  11.9 us
    dot_general x1, matrix products, body(): jnp.dot(mixed, lax.all_gather(out_weight, 'fsdp', axis=1, tiled=True), pr...  8.98 us
    convert_element_type x1, other arithmetic, body(): widened = states.astype(jnp.float32)  6.65 us
    all_to_all x1, waiting for transfers between devices, sent_to_all(): lax.all_to_all(jnp.broadcast_to(value[None], (length, *value.shape)), axi...  6.14 us
  transfers between devices with their start and end apart: 4, of which 4 were waited for; matrix products, arithmetic and copies ran while one was open for 10% of the time, Pallas kernels for 0%

commit v1 on v0

--- a/solution.py
+++ b/solution.py
@@ -127,7 +127,9 @@
     slice_cols = width // tensor_count
     partials = jnp.dot(
         mixed,
-        lax.all_gather(out_weight, "fsdp", axis=1, tiled=True),
+        jnp.concatenate(
+            lax.all_to_all(jnp.stack([out_weight] * lax.axis_size("fsdp")), "fsdp", 0, 0), axis=1
+        ),
         preferred_element_type=jnp.float32,
     )
     branch = lax.psum_scatter(partials, "tensor", scatter_dimension=1, tiled=True)

time: 299 us -> 336 us (1.12)
  waiting for transfers between devices: 236 us -> 260 us
  starting transfers between devices: 3.45 us -> 11.8 us
  local copies, waits for them, and re-layouts: 1.34 us -> 6.69 us
    all_gather x1, waiting for transfers between devices: 87.3 us -> 168 us  [in_one_piece(): result, at, outs = (lax.all_gather(both, axis, axis=dim, tiled=True), 0, [])]
    all_gather x1 -> x0, waiting for transfers between devices: 58.3 us -> none  [body(): lax.all_gather(out_weight, 'fsdp', axis=1, tiled=True)]
    all_to_all x0 -> x1, starting transfers between devices: none -> 8.34 us  [body(): lax.all_to_all(jnp.stack([out_weight] * lax.axis_size('fsdp')), 'fsdp', 0...]
    another operation x1 -> x2, local copies, waits for them, and re-layouts: 0.11 us -> 4.21 us  [the longest x1 4.09 us: body(): jnp.stack([out_weight] * lax.axis_size('fsdp'))]
  transfers between devices with their start and end apart: 4 -> 4, of which waited for: 4 -> 3; matrix products, arithmetic and copies ran while one was open for 10% -> 10% of each run, Pallas kernels for 0% -> 0%
where the time goes in v1:
time: 336 us; the launch traced here: 335 us
  waiting for transfers between devices  260 us (77%)
  matrix products  25.7 us (8%)
  other arithmetic  16.9 us (5%)
  between operations  14.2 us (4%)
  starting transfers between devices  11.8 us (4%)
  local copies, waits for them, and re-layouts  6.69 us (2%)
    all_gather x1, waiting for transfers between devices, in_one_piece(): result, at, outs = (lax.all_gather(both, axis, axis=dim, tiled=True), 0, [])  168 us
    reduce_scatter x1, waiting for transfers between devices, body(): lax.psum_scatter(partials, 'tensor', scatter_dimension=1, tiled=True)  86.4 us
    dot_general x2, matrix products, add_piece(): return jnp.dot(normed, portion, preferred_element_type=jnp.float32)  11.7 us
    dot_general x1, matrix products, body(): jnp.dot(mixed, jnp.concatenate(lax.all_to_all(jnp.stack([out_weight] * la...  9.02 us
    all_to_all x1, starting transfers between devices, body(): lax.all_to_all(jnp.stack([out_weight] * lax.axis_size('fsdp')), 'fsdp', 0...  8.34 us
  transfers between devices with their start and end apart: 4, of which 3 were waited for; matrix products, arithmetic and copies ran while one was open for 10% of the time, Pallas kernels for 0%

profile of v1, /device:TPU:0, one launch (start us, length us, event | category | flops | bytes accessed | tf_op | source)
XLA Modules:
  0.0 335.3 jit_solution(15507325769160504709)
XLA Ops:
  7.2 0.0 all-gather.2.cloned.1.call-start
  7.2 2.2 pad_maximum_fusion
  9.4 0.0 all-gather.2.cloned.1.call-update
  9.4 1.3 copy.31
  10.7 4.1 %stack.2 = bf16[16,512,512]{1,2,0:T(8,128)(2,1)} broadcast(bf16[512,512]{0,1:T(8,128)(2,1)S(1)} %copy.31), dimensions={1,2} | broadcast | bytes 8912896 | tf_op jit(solution)/shard_map/stack | solution.py:131
  14.7 0.0 copy-start
  14.8 0.0 copy-start.3
  14.8 8.3 %all-to-all-start = ((bf16[16,512,512]{1,2,0:T(8,128)(2,1)}), bf16[16,512,512]{1,2,0:T(8,128)(2,1)}, u32[]{:S(2)}, u32[]{:S(2)}) async-start(bf16[16,512,512]{1,2,0:T(8,128)(2,1)} %stack.2), calls=%async_computation | async-start | bytes 16777216 | tf_op jit(solution)/shard_map/all_to_all | solution.py:131
  23.1 0.0 reduce-scatter.2.cloned.1.call-start
  23.2 0.0 copy-done
  23.2 0.1 compare_reduce_fusion
  23.3 0.1 fusion.40
  23.3 0.3 reduce-window.9
  23.6 0.1 slice.47
  23.8 0.1 slice_reduce_fusion
  23.9 3.3 multiply_reduce_fusion
  27.2 0.1 fusion.41
  27.3 0.1 fusion.27
  27.4 0.5 multiply_cosine_fusion
  28.0 167.5 %all-gather.2.cloned.1.call-done = bf16[8192,768]{1,0:T(8,128)(2,1)} async-done(((bf16[512,768]{1,0:T(8,128)(2,1)}), bf16[8192,768]{1,0:T(8,128)(2,1)}) %all-gather.2.cloned.1.call-update) | async-done | bytes 12582928 | tf_op jit(solution)/shard_map/all_gather | solution.py:15
  195.5 0.0 copy-done.3
  195.5 7.0 %fusion = f32[256,512]{1,0:T(8,128)S(1)} fusion(bf16[8192,768]{1,0:T(8,128)(2,1)} %all-gather.2.cloned.1.call-done, f32[8192]{0:T(1024)S(1)} %copy-done.3, f32[256]{0:T(256)S(1)} %add_rsqrt_fusion, bf16[256,8192]{1,0:T(8,128)(2,1)} %param.9), kind=kOutput, calls=%fused_computation | convolution fusion | flops 2155872256 | bytes 13140992 | tf_op jit(solution)/shard_map/dot_general | solution.py:120
  202.5 0.2 reshape.259
  202.7 4.6 %fusion.8 = f32[256,1,128]{0,2,1:T(8,128)S(1)} fusion(bf16[8192,768]{1,0:T(8,128)(2,1)} %all-gather.2.cloned.1.call-done, f32[8192]{0:T(1024)S(1)} %copy-done.3, f32[256]{0:T(256)S(1)} %add_rsqrt_fusion, bf16[256,8192]{1,0:T(8,128)(2,1)} %param.9), kind=kOutput, calls=%fused_computation.14 | convolution fusion | flops 545259520 | bytes 6456320 | tf_op jit(solution)/shard_map/dot_general | solution.py:120
  207.3 0.3 fusion.39
  207.6 0.3 fusion.43
  208.0 0.1 subtract_convert_fusion
  208.1 0.4 fusion.45
  208.6 0.2 fusion.21
  208.7 4.6 %convolution_convert_fusion = bf16[128,4,256]{2,0,1:T(8,128)(2,1)S(1)} fusion(bf16[8192,768]{1,0:T(8,128)(2,1)} %all-gather.2.cloned.1.call-done, f32[1,4,256,256]{2,3,1,0:T(8,128)S(1)} %get-tuple-element.16, f32[4,256]{1,0:T(4,128)S(1)} %fusion.21, f32[4,256]{1,0:T(4,128)S(1)} %get-tuple-element.15, f32[8192]{0:T(1024)S(1)} %copy-done.3, ...), kind=kOutput, calls=%fused_computation.13 | convolution fusion | flops 613318656 | bytes 7644160 | tf_op jit(solution)/shard_map/kgts,skd->tkgd/dot_general | solution.py:92
  213.3 0.0 all-to-all-done
  213.3 9.0 %fusion.46 = f32[256,8192]{1,0:T(8,128)} fusion(bf16[256,512]{0,1:T(8,128)(2,1)S(1)} %bitcast.43, bf16[512,8192]{0,1:T(8,128)(2,1)} %bitcast.15), kind=kOutput, calls=%fused_computation.64 | convolution fusion | flops 2147483648 | bytes 17039360 | tf_op jit(solution)/shard_map/dot_general | solution.py:128
  222.3 0.0 reduce-scatter.2.cloned.1.call-update
  222.4 0.0 copy-start.1
  222.4 0.0 copy-start.2
  222.4 6.4 %convert_element_type.41 = f32[256,8192]{1,0:T(8,128)} convert(bf16[256,8192]{1,0:T(8,128)(2,1)} %param.9) | non-fusion elementwise | flops 2097152 | bytes 12582912 | tf_op jit(solution)/shard_map/convert_element_type | solution.py:112
  228.8 0.0 copy-done.1
  228.8 0.0 copy-done.2
  228.8 86.4 %reduce-scatter.2.cloned.1.call-done = f32[256,1024]{1,0:T(8,128)} async-done(((f32[256,8192]{1,0:T(8,128)}), f32[256,1024]{1,0:T(8,128)}) %reduce-scatter.2.cloned.1.call-update) | async-done | bytes 1048592 | tf_op jit(solution)/shard_map/reduce_scatter | solution.py:135
  315.2 2.5 fusion.19
  317.8 0.6 broadcast_in_dim.15
  318.4 3.3 all-to-all-start.1
  321.7 6.1 %all-to-all-done.1 = f32[8,1,512]{2,1,0:T(1,128)S(1)} async-done(((f32[8,1,512]{2,1,0:T(1,128)}), f32[8,1,512]{2,1,0:T(1,128)S(1)}, u32[]{:S(2)}, u32[]{:S(2)}) %all-to-all-start.1) | async-done | bytes 16416 | tf_op jit(solution)/shard_map/all_to_all | solution.py:24
  327.9 0.6 rsqrt_multiply_fusion
  (7 shorter events, 0.1 us)
Async XLA Ops:
  7.2 188.3 %all-gather.2.cloned.1.call-start = ((), (), s32[]{:S(2)}) async-start(), calls=%async_computation.3 | async-start | bytes 13369344 | tf_op jit(solution)/shard_map/all_gather | solution.py:15
  14.7 8.4 %copy-start = (s32[1,256]{1,0:T(1,128)S(1)}, s32[1,256]{1,0:T(1,128)}, u32[]{:S(2)}) copy-start(s32[1,256]{1,0:T(1,128)} %param.10) | copy-start | bytes 3076
  14.8 180.7 %copy-start.3 = (f32[8192]{0:T(1024)S(1)}, f32[8192]{0:T(1024)}, u32[]{:S(2)}) copy-start(f32[8192]{0:T(1024)} %param.11) | copy-start | bytes 98308
  14.8 198.6 %all-to-all-start = ((bf16[16,512,512]{1,2,0:T(8,128)(2,1)}), bf16[16,512,512]{1,2,0:T(8,128)(2,1)}, u32[]{:S(2)}, u32[]{:S(2)}) async-start(bf16[16,512,512]{1,2,0:T(8,128)(2,1)} %stack.2), calls=%async_computation | async-start | bytes 16777216 | tf_op jit(solution)/shard_map/all_to_all | solution.py:131
  23.1 292.1 %reduce-scatter.2.cloned.1.call-start = ((), (), s32[]{:S(2)}) async-start(), calls=%async_computation.4 | async-start | bytes 9437184 | tf_op jit(solution)/shard_map/reduce_scatter | solution.py:135
  222.4 6.4 %copy-start.1 = (f32[1024]{0:T(1024)S(1)}, f32[1024]{0:T(1024)}, u32[]{:S(2)}) copy-start(f32[1024]{0:T(1024)} %param.16) | copy-start | bytes 12292
  222.4 6.4 %copy-start.2 = (f32[1024]{0:T(1024)S(1)}, f32[1024]{0:T(1024)}, u32[]{:S(2)}) copy-start(f32[1024]{0:T(1024)} %param.17) | copy-start | bytes 12292
  318.4 9.5 %all-to-all-start.1 = ((f32[8,1,512]{2,1,0:T(1,128)}), f32[8,1,512]{2,1,0:T(1,128)S(1)}, u32[]{:S(2)}, u32[]{:S(2)}) async-start(f32[8,1,512]{2,1,0:T(1,128)} %broadcast_in_dim.15), calls=%async_computation.2 | async-start | bytes 32768 | tf_op jit(solution)/shard_map/all_to_all | solution.py:24
Sparse Core Ops, SparseCore 0:
  10.5 184.9 all-gather.1
  222.5 92.7 reduce-scatter.1
